TPU v7x, 32 devices: a whole 2x2x4 slice. The times are simulated.
32 devices in a mesh: dp: 2 (over x), fsdp: 16 (over z, y, core).
Axes of the slice: x: 2, y: 2, z: 4, core: 2. Of those that a mesh axis runs over, the one named last changes fastest.
Arguments:
- hidden_states: bfloat16 [32, 1024, 768], P(('dp', 'fsdp')), may hold values from -6 to 6
- condition: bfloat16 [32, 128], P(('dp', 'fsdp')), may hold values from -6 to 6
- absorbed: int32 [32, 1024], P(('dp', 'fsdp')), may hold values 0 or 1
- positions: int32 [32, 1024], P(('dp', 'fsdp')), may hold values from 0 to 2047, as said below
- modulator: bfloat16 [128, 4608], P('fsdp'), may hold values from -0.5 to 0.5
- offsets: bfloat16 [4608], P('fsdp'), may hold values from -3 to 3
- prescale: bfloat16 [768], P('fsdp'), may hold values from 0.5 to 1.5
- projector: bfloat16 [768, 2304], P('fsdp'), may hold values from -0.3125 to 0.3125
- merger: bfloat16 [768, 768], P('fsdp'), may hold values from -0.625 to 0.625
- midscale: bfloat16 [768], P('fsdp'), may hold values from 0.5 to 1.5
- expander: bfloat16 [768, 3072], P('fsdp'), may hold values from -0.21875 to 0.21875
- thresholds: bfloat16 [3072], P('fsdp'), may hold values from -3 to 3
- contractor: bfloat16 [3072, 768], P('fsdp'), may hold values from -0.109375 to 0.109375
- baseline: bfloat16 [768], P('fsdp'), may hold values from -3 to 3
- absorber: bfloat16 [768], P('fsdp'), may hold values from -6 to 6
- cotangent: bfloat16 [32, 1024, 768], P(('dp', 'fsdp')), may hold values from -6 to 6
Outputs:
- block_output: bfloat16 [32, 1024, 768], P(('dp', 'fsdp'))
- grad_hidden: float32 [32, 1024, 768], P(('dp', 'fsdp'))
- grad_condition: float32 [32, 128], P(('dp', 'fsdp'))
- grad_modulator: float32 [128, 4608], P('fsdp')
- grad_offsets: float32 [4608], P('fsdp')
- grad_prescale: float32 [768], P('fsdp')
- grad_projector: float32 [768, 2304], P('fsdp')
- grad_merger: float32 [768, 768], P('fsdp')
- grad_midscale: float32 [768], P('fsdp')
- grad_expander: float32 [768, 3072], P('fsdp')
- grad_thresholds: float32 [3072], P('fsdp')
- grad_contractor: float32 [3072, 768], P('fsdp')
- grad_baseline: float32 [768], P('fsdp')
- grad_absorber: float32 [768], P('fsdp')
Inputs may be any that keep to these rules, and one draw needn't show every extreme that they name: `absorbed`: 1 marks a token in the absorbing state, 0 any other. Along each sequence the positions rise by 1 or 2 from one token to the next; the first is 0 or 1. The first sequence starts at 0, and the last sequence rises by 2 at every token.
All inputs are finite; a program needn't handle non-finite values. No bound on the sum of `absorbed` on one device may be relied on, other than what follows from the above.
Results may differ from a plain program's by a relative error of at most 0.039.
Values may be sent and summed in bfloat16 or wider, within the bound.
A program may use at most 192 MiB of HBM per device.

v0:
```python
import jax
import jax.numpy as jnp
from jax import lax
from jax.sharding import PartitionSpec as P

D = 768
HEADS = 12
HD = 64


def norm_shift(values, gain, shift, scale):
    mean = jnp.mean(values, -1, keepdims=True)
    centered = values - mean
    variance = jnp.mean(centered * centered, -1, keepdims=True)
    return centered * lax.rsqrt(variance + 1e-05) * gain * (1.0 + scale) + shift


def rotate(values, cosine, sine):
    half = values.shape[-1] // 2
    first = values[..., :half]
    second = values[..., half:]
    return jnp.concatenate([first * cosine - second * sine, second * cosine + first * sine], -1)


def unrotate(grads, cosine, sine):
    half = grads.shape[-1] // 2
    first = grads[..., :half]
    second = grads[..., half:]
    return jnp.concatenate([first * cosine + second * sine, second * cosine - first * sine], -1)


def gelu_tanh(values):
    return jax.nn.gelu(values, approximate=True)


def head_scores(queries, keys):
    factor = queries.shape[-1] ** (-0.5)
    return jnp.einsum("sqd,skd->sqk", queries, keys, preferred_element_type=jnp.float32) * factor


def attend_head(operands):
    queries, keys, values = operands
    scores = head_scores(queries, keys)
    top = jnp.max(scores, -1, keepdims=True)
    expo = jnp.exp(scores - top)
    total = jnp.sum(expo, -1, keepdims=True)
    probs = (expo / total).astype(jnp.bfloat16)
    mixed = jnp.einsum("sqk,skd->sqd", probs, values, preferred_element_type=jnp.float32)
    return (mixed, (top + jnp.log(total))[..., 0])


def head_grads(operands):
    queries, keys, values, upstream, logsum = operands
    factor = queries.shape[-1] ** (-0.5)
    scores = head_scores(queries, keys)
    probs = jnp.exp(scores - logsum[..., None])
    dprobs = jnp.einsum("sqd,skd->sqk", upstream, values, preferred_element_type=jnp.float32)
    score_grad = (probs * (dprobs - jnp.sum(dprobs * probs, -1, keepdims=True))).astype(
        jnp.bfloat16
    )
    query_grad = (
        jnp.einsum("sqk,skd->sqd", score_grad, keys, preferred_element_type=jnp.float32) * factor
    )
    key_grad = (
        jnp.einsum("sqk,sqd->skd", score_grad, queries, preferred_element_type=jnp.float32) * factor
    )
    value_grad = jnp.einsum(
        "sqk,sqd->skd", probs.astype(jnp.bfloat16), upstream, preferred_element_type=jnp.float32
    )
    return (query_grad, key_grad, value_grad)


def shards(
    hidden_states,
    condition,
    absorbed,
    positions,
    modulator,
    offsets,
    prescale,
    projector,
    merger,
    midscale,
    expander,
    thresholds,
    contractor,
    baseline,
    absorber,
    cotangent,
):
    gathered = (
        lax.all_gather(modulator, "fsdp", axis=0, tiled=True),
        lax.all_gather(offsets, "fsdp", axis=0, tiled=True),
        lax.all_gather(prescale, "fsdp", axis=0, tiled=True),
        lax.all_gather(projector, "fsdp", axis=0, tiled=True),
        lax.all_gather(merger, "fsdp", axis=0, tiled=True),
        lax.all_gather(midscale, "fsdp", axis=0, tiled=True),
        lax.all_gather(expander, "fsdp", axis=0, tiled=True),
        lax.all_gather(thresholds, "fsdp", axis=0, tiled=True),
        lax.all_gather(contractor, "fsdp", axis=0, tiled=True),
        lax.all_gather(baseline, "fsdp", axis=0, tiled=True),
        lax.all_gather(absorber, "fsdp", axis=0, tiled=True),
    )
    (
        full_modulator,
        full_offsets,
        full_prescale,
        full_projector,
        full_merger,
        full_midscale,
        full_expander,
        full_thresholds,
        full_contractor,
        full_baseline,
        full_absorber,
    ) = gathered
    sequences = hidden_states.shape[0]
    length = hidden_states.shape[1]
    mask_rows = (absorbed == 1)[..., None]
    block_in = jnp.where(
        mask_rows, full_absorber.astype(jnp.float32), hidden_states.astype(jnp.float32)
    )
    cond_float = condition.astype(jnp.float32)
    silu_cond = jax.nn.silu(cond_float).astype(jnp.bfloat16)
    modulation = (
        jnp.dot(silu_cond, full_modulator, preferred_element_type=jnp.float32) + full_offsets
    )
    shift_one, scale_one, gate_one, shift_two, scale_two, gate_two = jnp.split(
        modulation[:, None, :], 6, axis=-1
    )
    normed_one = (
        norm_shift(block_in, full_prescale, shift_one, scale_one)
        .astype(jnp.bfloat16)
        .reshape(-1, D)
    )
    united = jnp.dot(normed_one, full_projector, preferred_element_type=jnp.float32)
    half = HD // 2
    inverse = 10000.0 ** (-jnp.arange(half, dtype=jnp.float32) / half)
    angles = positions.astype(jnp.float32)[..., None] * inverse
    cosine = jnp.cos(angles)
    sine = jnp.sin(angles)
    heads_view = united.reshape(sequences, length, 3, HEADS, HD).transpose(2, 3, 0, 1, 4)
    queries = rotate(heads_view[0], cosine, sine).astype(jnp.bfloat16)
    keys = rotate(heads_view[1], cosine, sine).astype(jnp.bfloat16)
    values = heads_view[2].astype(jnp.bfloat16)
    mixed, logsum = lax.map(attend_head, (queries, keys, values))
    attended = mixed.transpose(1, 2, 0, 3).reshape(-1, D).astype(jnp.bfloat16)
    branch_one = jnp.dot(attended, full_merger, preferred_element_type=jnp.float32).reshape(
        sequences, length, D
    )
    middle = block_in + gate_one * branch_one
    normed_two = (
        norm_shift(middle, full_midscale, shift_two, scale_two).astype(jnp.bfloat16).reshape(-1, D)
    )
    expanded = (
        jnp.dot(normed_two, full_expander, preferred_element_type=jnp.float32) + full_thresholds
    )
    activated = gelu_tanh(expanded).astype(jnp.bfloat16)
    branch_two = (
        jnp.dot(activated, full_contractor, preferred_element_type=jnp.float32) + full_baseline
    ).reshape(sequences, length, D)
    block_output = (middle + gate_two * branch_two).astype(jnp.bfloat16)
    gathered = (
        lax.all_gather(modulator, "fsdp", axis=0, tiled=True),
        lax.all_gather(offsets, "fsdp", axis=0, tiled=True),
        lax.all_gather(prescale, "fsdp", axis=0, tiled=True),
        lax.all_gather(projector, "fsdp", axis=0, tiled=True),
        lax.all_gather(merger, "fsdp", axis=0, tiled=True),
        lax.all_gather(midscale, "fsdp", axis=0, tiled=True),
        lax.all_gather(expander, "fsdp", axis=0, tiled=True),
        lax.all_gather(thresholds, "fsdp", axis=0, tiled=True),
        lax.all_gather(contractor, "fsdp", axis=0, tiled=True),
        lax.all_gather(baseline, "fsdp", axis=0, tiled=True),
        lax.all_gather(absorber, "fsdp", axis=0, tiled=True),
    )
    (
        full_modulator,
        full_offsets,
        full_prescale,
        full_projector,
        full_merger,
        full_midscale,
        full_expander,
        full_thresholds,
        full_contractor,
        full_baseline,
        full_absorber,
    ) = gathered
    upstream = cotangent.astype(jnp.float32)
    grad_gate_two = jnp.sum(upstream * branch_two, axis=1)
    branch_grad = (upstream * gate_two).astype(jnp.bfloat16).reshape(-1, D)
    grad_baseline = jnp.sum(branch_grad, 0, dtype=jnp.float32)
    grad_contractor = jnp.einsum(
        "tf,td->fd", activated, branch_grad, preferred_element_type=jnp.float32
    )
    activated_grad = jnp.einsum(
        "td,fd->tf", branch_grad, full_contractor, preferred_element_type=jnp.float32
    )
    unused_value, gelu_back = jax.vjp(gelu_tanh, expanded)
    expand_grad = gelu_back(activated_grad)[0].astype(jnp.bfloat16)
    grad_thresholds = jnp.sum(expand_grad, 0, dtype=jnp.float32)
    grad_expander = jnp.einsum(
        "td,tf->df", normed_two, expand_grad, preferred_element_type=jnp.float32
    )
    normed_two_grad = jnp.einsum(
        "tf,df->td", expand_grad, full_expander, preferred_element_type=jnp.float32
    ).reshape(sequences, length, D)
    unused_value, second_back = jax.vjp(
        norm_shift, middle, full_midscale.astype(jnp.float32), shift_two, scale_two
    )
    middle_grad, grad_midscale, grad_shift_two, grad_scale_two = second_back(normed_two_grad)
    middle_grad = middle_grad + upstream
    grad_gate_one = jnp.sum(middle_grad * branch_one, axis=1)
    merged_grad = (middle_grad * gate_one).astype(jnp.bfloat16).reshape(-1, D)
    grad_merger = jnp.einsum("td,te->de", attended, merged_grad, preferred_element_type=jnp.float32)
    attended_grad = jnp.einsum(
        "te,de->td", merged_grad, full_merger, preferred_element_type=jnp.float32
    ).astype(jnp.bfloat16)
    upstream_heads = attended_grad.reshape(sequences, length, HEADS, HD).transpose(2, 0, 1, 3)
    query_grad, key_grad, value_grad = lax.map(
        head_grads, (queries, keys, values, upstream_heads, logsum)
    )
    query_grad = unrotate(query_grad, cosine, sine)
    key_grad = unrotate(key_grad, cosine, sine)
    united_grad = (
        jnp.stack([query_grad, key_grad, value_grad])
        .transpose(2, 3, 0, 1, 4)
        .reshape(-1, 3 * D)
        .astype(jnp.bfloat16)
    )
    grad_projector = jnp.einsum(
        "td,te->de", normed_one, united_grad, preferred_element_type=jnp.float32
    )
    normed_one_grad = jnp.einsum(
        "te,de->td", united_grad, full_projector, preferred_element_type=jnp.float32
    ).reshape(sequences, length, D)
    unused_value, first_back = jax.vjp(
        norm_shift, block_in, full_prescale.astype(jnp.float32), shift_one, scale_one
    )
    input_grad, grad_prescale, grad_shift_one, grad_scale_one = first_back(normed_one_grad)
    input_grad = input_grad + middle_grad
    grad_hidden = jnp.where(mask_rows, 0.0, input_grad)
    grad_absorber = jnp.sum(jnp.where(mask_rows, input_grad, 0.0), axis=(0, 1))
    modulation_grad = jnp.concatenate(
        [
            grad_shift_one[:, 0],
            grad_scale_one[:, 0],
            grad_gate_one,
            grad_shift_two[:, 0],
            grad_scale_two[:, 0],
            grad_gate_two,
        ],
        -1,
    )
    grad_offsets = jnp.sum(modulation_grad, 0)
    grad_modulator = jnp.dot(
        silu_cond.astype(jnp.float32).T, modulation_grad, precision=lax.Precision.HIGHEST
    )
    silu_grad = jnp.dot(
        modulation_grad, full_modulator.astype(jnp.float32).T, precision=lax.Precision.HIGHEST
    )
    unused_value, silu_back = jax.vjp(jax.nn.silu, cond_float)
    grad_condition = silu_back(silu_grad)[0]
    scattered = (
        lax.psum_scatter(grad_modulator, "fsdp", scatter_dimension=0, tiled=True),
        lax.psum_scatter(grad_offsets, "fsdp", scatter_dimension=0, tiled=True),
        lax.psum_scatter(grad_prescale, "fsdp", scatter_dimension=0, tiled=True),
        lax.psum_scatter(grad_projector, "fsdp", scatter_dimension=0, tiled=True),
        lax.psum_scatter(grad_merger, "fsdp", scatter_dimension=0, tiled=True),
        lax.psum_scatter(grad_midscale, "fsdp", scatter_dimension=0, tiled=True),
        lax.psum_scatter(grad_expander, "fsdp", scatter_dimension=0, tiled=True),
        lax.psum_scatter(grad_thresholds, "fsdp", scatter_dimension=0, tiled=True),
        lax.psum_scatter(grad_contractor, "fsdp", scatter_dimension=0, tiled=True),
        lax.psum_scatter(grad_baseline, "fsdp", scatter_dimension=0, tiled=True),
        lax.psum_scatter(grad_absorber, "fsdp", scatter_dimension=0, tiled=True),
    )
    summed = (
        lax.psum(scattered[0].astype(jnp.bfloat16), "dp").astype(jnp.float32),
        lax.psum(scattered[1].astype(jnp.bfloat16), "dp").astype(jnp.float32),
        lax.psum(scattered[2].astype(jnp.bfloat16), "dp").astype(jnp.float32),
        lax.psum(scattered[3].astype(jnp.bfloat16), "dp").astype(jnp.float32),
        lax.psum(scattered[4].astype(jnp.bfloat16), "dp").astype(jnp.float32),
        lax.psum(scattered[5].astype(jnp.bfloat16), "dp").astype(jnp.float32),
        lax.psum(scattered[6].astype(jnp.bfloat16), "dp").astype(jnp.float32),
        lax.psum(scattered[7].astype(jnp.bfloat16), "dp").astype(jnp.float32),
        lax.psum(scattered[8].astype(jnp.bfloat16), "dp").astype(jnp.float32),
        lax.psum(scattered[9].astype(jnp.bfloat16), "dp").astype(jnp.float32),
        lax.psum(scattered[10].astype(jnp.bfloat16), "dp").astype(jnp.float32),
    )
    return (
        block_output,
        grad_hidden,
        grad_condition,
        summed[0],
        summed[1],
        summed[2],
        summed[3],
        summed[4],
        summed[5],
        summed[6],
        summed[7],
        summed[8],
        summed[9],
        summed[10],
    )


def solution(mesh):
    return jax.shard_map(
        shards,
        mesh=mesh,
        in_specs=(
            P(("dp", "fsdp"), None, None),
            P(("dp", "fsdp"), None),
            P(("dp", "fsdp"), None),
            P(("dp", "fsdp"), None),
            P("fsdp", None),
            P("fsdp"),
            P("fsdp"),
            P("fsdp", None),
            P("fsdp", None),
            P("fsdp"),
            P("fsdp", None),
            P("fsdp"),
            P("fsdp", None),
            P("fsdp"),
            P("fsdp"),
            P(("dp", "fsdp"), None, None),
        ),
        out_specs=(
            P(("dp", "fsdp"), None, None),
            P(("dp", "fsdp"), None, None),
            P(("dp", "fsdp"), None),
            P("fsdp", None),
            P("fsdp"),
            P("fsdp"),
            P("fsdp", None),
            P("fsdp", None),
            P("fsdp"),
            P("fsdp", None),
            P("fsdp"),
            P("fsdp", None),
            P("fsdp"),
            P("fsdp"),
        ),
        check_vma=False,
    )
```

profile of v0, /device:TPU:0, one launch (start us, length us, event | category | flops | bytes accessed | tf_op | source)
XLA Modules:
  0.0 929.5 jit_solution(9982716216045401141)
XLA Ops:
  20.4 63.4 %all-reduce.13 = (bf16[4608]{0:T(1024)(128)(2,1)S(1)}, bf16[768]{0:T(1024)(128)(2,1)S(1)}, bf16[768]{0:T(1024)(128)(2,1)S(1)}, bf16[768]{0:T(1024)(128)(2,1)S(1)...) all-reduce(bf16[4608]{0:T(1024)(128)(2,1)S(1)} %dynamic-update-slic, ...), channel_id=1, replica_groups=mesh['dp'=2,'fsdp'=16] {'fsdp'}, use_global_device_ids=true, to_apply=%add.1 | all-reduce | flops 10752 | bytes 43008
  86.0 2.7 copy.69
  91.5 8.6 all-gather.8.cloned.1.call-done
  100.1 5.7 copy.43
  105.9 6.3 fusion.74
  117.6 3.1 copy.45
  120.6 4.1 copy.46
  124.7 4.1 copy.47
  128.9 60.6 %while.28 = (s32[]{:T(128)}, bf16[12,1,1024,64]{2,3,1,0:T(8,128)(2,1)}, f32[12,1,1024]{2,1,0:T(1,128)S(1)}, bf16[12,1,1024,64]{3,2,1,0:T(8,128)(2,1)S(1)}, bf16[...) while((s32[]{:T(128)}, bf16[12,1,1024,64]{2,3,1,0:T(8,128)(2,1)}, ...), condition=%wide.region_5.6_spmd.clone, body=%wide.region_2.5_spmd.sunk.clone | while | flops 277871616 | bytes 13674569 | solution.py:146
  146.6 2.6 fusion.157
  189.5 5.7 fusion.102
  197.4 14.9 %multiply_convert_fusion.1 = (bf16[1024,3072]{1,0:T(8,128)(2,1)}, f32[1024,3072]{1,0:T(8,128)}) fusion(f32[3072]{0:T(1024)S(1)} %convert_element_type.211, bf16[768,3072]{1,0:T(8,128)(2,1)} %all-gather.12.cloned.1.call-done, f32[1,1024,768]{2,1,0:T(8,128)} %copy-done, f32[768]{0:T(1024)S(1)} %get-tuple-element.140, f32[768]{0:T(1024)S(1)} %get-tuple-element.141, ...), kind=kOutput, calls=%fused_computation.65 | convolution fusion | flops 4868014080 | bytes 26768384 | tf_op jit(solution)/shard_map/dot_general | solution.py:156
  212.2 35.2 %all-gather.14.cloned.1.call-done = bf16[3072,768]{1,0:T(8,128)(2,1)} async-done(((bf16[192,768]{1,0:T(8,128)(2,1)}), bf16[3072,768]{1,0:T(8,128)(2,1)}) %all-gather.14.cloned.1.call-update) | async-done | bytes 4718608 | tf_op jit(solution)/shard_map/all_gather | solution.py:100
  247.4 16.7 %convert_reduce_fusion = (f32[3072]{0:T(1024)S(1)}, bf16[1024,3072]{1,0:T(8,128)(2,1)S(1)}) fusion(f32[1024,3072]{1,0:T(8,128)} %get-tuple-element.233, f32[3072]{0:T(1024)S(1)} %convert_element_type.211, bf16[3072,768]{1,0:T(8,128)(2,1)} %all-gather.14.cloned.1.call-done, bf16[1,1024,768]{2,1,0:T(8,128)(2,1)} %param.35, f32[768]{0:T(1024)S(1)} %get-tuple-element.139), kind=kOutput, calls=%fused_computation.64 | convolution fusion | flops 4906546176 | bytes 25193472 | tf_op jit(solution)/shard_map/td,fd->tf/dot_general | solution.py:196
  264.2 5.9 fusion.58
  270.1 10.2 %fusion.57 = (f32[768]{0:T(1024)S(1)}, bf16[1,1024,768]{2,1,0:T(8,128)(2,1)}, f32[1024]{0:T(1024)S(1)}, f32[1,1024,768]{2,1,0:T(8,128)S(1)}) fusion(bf16[1,1024,768]{2,1,0:T(8,128)(2,1)S(1)} %copy-done.8, f32[768]{0:T(1024)S(1)} %convert_element_type.213, f32[1,1024,768]{2,1,0:T(8,128)S(1)} %copy-done.1, f32[768]{0:T(1024)S(1)} %get-tuple-element.139, ...), kind=kOutput, calls=%fused_computation.73 | convolution fusion | flops 4843632640 | bytes 23624704 | tf_op jit(solution)/shard_map/dot_general | solution.py:160
  282.4 4.2 fusion.81
  286.6 4.8 convolution_convert_fusion
  291.4 4.6 copy.48
  296.0 131.9 %while.29 = (s32[]{:T(128)}, f32[12,1,1024,64]{2,3,1,0:T(8,128)}, f32[12,1,1024,64]{2,3,1,0:T(8,128)}, bf16[12,1,1024,64]{2,3,1,0:T(8,128)(2,1)}, bf16[12,1,1024...) while((s32[]{:T(128)}, f32[12,1,1024,64]{2,3,1,0:T(8,128)}, ...), condition=%wide.region_12.13_spmd.clone, body=%wide.region_10.12_spmd.sunk.clone | while | flops 683801600 | bytes 34112608 | solution.py:220
  427.9 3.9 multiply_add_fusion.1
  436.1 6.7 fusion.59
  447.1 3.3 fusion.100
  455.2 9.9 %fusion.76 = f32[768,2304]{1,0:T(8,128)} fusion(bf16[1024,2304]{0,1:T(8,128)(2,1)} %bitcast.248, bf16[1,1024,768]{2,1,0:T(8,128)(2,1)S(1)} %copy-done.4, f32[768]{0:T(1024)S(1)} %copy-done.31, f32[768]{0:T(1024)S(1)} %copy-done.28, f32[768]{0:T(1024)S(1)} %copy-done.26, f32[1024]{0:T(1024)S(1)} %copy-done.24, f32[1024]{0:T(1024)S(1)} %copy-done.20, ...), kind=kOutput, calls=%fused_computation.118 | convolution fusion | flops 3630170112 | bytes 13390848 | tf_op jit(solution)/shard_map/td,te->de/dot_general | solution.py:231
  467.0 10.8 %fusion.96 = f32[768,3072]{1,0:T(8,128)} fusion(bf16[1024,3072]{1,0:T(8,128)(2,1)} %copy-done.7, f32[1,1024,768]{2,1,0:T(8,128)S(1)} %copy-done.2, f32[768]{0:T(1024)S(1)} %get-tuple-element.140, f32[768]{0:T(1024)S(1)} %get-tuple-element.141, f32[768]{0:T(1024)S(1)} %convert_element_type.209, f32[1024]{0:T(1024)S(1)} %fusion.87, ...), kind=kOutput, calls=%fused_computation.178 | convolution fusion | flops 4836556800 | bytes 18891776 | tf_op jit(solution)/shard_map/td,tf->df/dot_general | solution.py:202
  479.3 10.5 %fusion.78 = f32[3072,768]{1,0:T(8,128)} fusion(bf16[1024,3072]{1,0:T(8,128)(2,1)} %get-tuple-element.232, bf16[1,1024,768]{2,1,0:T(8,128)(2,1)S(1)} %copy-done.9, f32[768]{0:T(1024)S(1)} %get-tuple-element.139), kind=kOutput, calls=%fused_computation.129 | convolution fusion | flops 4834197504 | bytes 17304576 | tf_op jit(solution)/shard_map/tf,td->fd/dot_general | solution.py:193
  491.5 25.5 %reduce-scatter.6.cloned.1.call-done = f32[8,4608]{1,0:T(8,128)} async-done(((f32[128,4608]{1,0:T(8,128)}), f32[8,4608]{1,0:T(8,128)}) %reduce-scatter.6.cloned.1.call-update) | async-done | bytes 147472 | tf_op jit(solution)/shard_map/reduce_scatter | solution.py:265
  518.6 91.4 %reduce-scatter.8.cloned.1.call-done = f32[48,2304]{1,0:T(8,128)} async-done(((f32[768,2304]{1,0:T(8,128)}), f32[48,2304]{1,0:T(8,128)}) %reduce-scatter.8.cloned.1.call-update) | async-done | bytes 442384 | tf_op jit(solution)/shard_map/reduce_scatter | solution.py:268
  611.7 113.3 %reduce-scatter.12.cloned.1.call-done = f32[48,3072]{1,0:T(8,128)} async-done(((f32[768,3072]{1,0:T(8,128)}), f32[48,3072]{1,0:T(8,128)}) %reduce-scatter.12.cloned.1.call-update) | async-done | bytes 589840 | tf_op jit(solution)/shard_map/reduce_scatter | solution.py:271
  726.8 113.0 %reduce-scatter.14.cloned.1.call-done = f32[192,768]{1,0:T(8,128)} async-done(((f32[3072,768]{1,0:T(8,128)}), f32[192,768]{1,0:T(8,128)}) %reduce-scatter.14.cloned.1.call-update) | async-done | bytes 589840 | tf_op jit(solution)/shard_map/reduce_scatter | solution.py:273
  843.9 60.3 %all-reduce.12 = (bf16[4608]{0:T(1024)(128)(2,1)S(1)}, bf16[768]{0:T(1024)(128)(2,1)S(1)}, bf16[768]{0:T(1024)(128)(2,1)S(1)}, bf16[3072]{0:T(1024)(128)(2,1)S(1...) all-reduce(f32[4608]{0:T(1024)S(1)} %reduce.32, ...), channel_id=3, replica_groups=mesh['dp'=2,'fsdp'=16] {'fsdp'}, use_global_device_ids=true, to_apply=%region_23.24.clone | all-reduce | flops 10752 | bytes 64512
  904.6 4.9 all-reduce.14
  (330 shorter events, 254.3 us)
Async XLA Ops:
  7.2 77.3 %copy-start.3 = (bf16[1,1024,768]{2,1,0:T(8,128)(2,1)S(1)}, bf16[1,1024,768]{2,1,0:T(8,128)(2,1)}, u32[]{:S(2)}) copy-start(bf16[1,1024,768]{2,1,0:T(8,128)(2,1)} %param.20) | copy-start | bytes 4718596
  7.2 78.8 %copy-start.29 = (s32[1,1024]{1,0:T(1,128)S(1)}, s32[1,1024]{1,0:T(1,128)}, u32[]{:S(2)}) copy-start(s32[1,1024]{1,0:T(1,128)} %param.23) | copy-start | bytes 12292
  7.2 82.6 %all-gather.6.cloned.1.call-start = ((), (), s32[]{:S(2)}) async-start(), calls=%async_computation.5 | async-start | bytes 1253376 | tf_op jit(solution)/shard_map/all_gather | solution.py:92
  7.9 92.2 %all-gather.8.cloned.1.call-start = ((), (), s32[]{:S(2)}) async-start(), calls=%async_computation.6 | async-start | bytes 3760128 | tf_op jit(solution)/shard_map/all_gather | solution.py:95
  8.7 180.8 %all-gather.10.cloned.1.call-start = ((), (), s32[]{:S(2)}) async-start(), calls=%async_computation.7 | async-start | bytes 1253376 | tf_op jit(solution)/shard_map/all_gather | solution.py:96
  9.4 187.9 %all-gather.12.cloned.1.call-start = ((), (), s32[]{:S(2)}) async-start(), calls=%async_computation.8 | async-start | bytes 5013504 | tf_op jit(solution)/shard_map/all_gather | solution.py:98
  10.0 237.4 %all-gather.14.cloned.1.call-start = ((), (), s32[]{:S(2)}) async-start(), calls=%async_computation.9 | async-start | bytes 5013504 | tf_op jit(solution)/shard_map/all_gather | solution.py:100
  10.6 479.3 %reduce-scatter.10.cloned.1.call-start = ((), (), s32[]{:S(2)}) async-start(), calls=%async_computation.12 | async-start | bytes 2506752 | tf_op jit(solution)/shard_map/reduce_scatter | solution.py:269
  84.5 4.2 copy-start.32
  85.1 20.8 %copy-start.19 = (f32[1024]{0:T(1024)}, f32[1024]{0:T(1024)S(1)}, u32[]{:S(2)}) copy-start(f32[1024]{0:T(1024)S(1)} %broadcast_multiply_fusion.2) | copy-start | bytes 12292
  85.9 19.9 %copy-start.23 = (f32[1024]{0:T(1024)}, f32[1024]{0:T(1024)S(1)}, u32[]{:S(2)}) copy-start(f32[1024]{0:T(1024)S(1)} %fusion.86) | copy-start | bytes 12292
  86.0 19.9 %copy-start.25 = (f32[768]{0:T(1024)}, f32[768]{0:T(1024)S(1)}, u32[]{:S(2)}) copy-start(f32[768]{0:T(1024)S(1)} %convert_element_type.202) | copy-start | bytes 9220
  89.8 24.6 %copy-start.15 = (f32[1024,32]{0,1:T(8,128)}, f32[1024,32]{0,1:T(8,128)S(1)}, u32[]{:S(2)}) copy-start(f32[1024,32]{0,1:T(8,128)S(1)} %get-tuple-element.227) | copy-start | bytes 393220
  89.8 24.6 %copy-start.17 = (f32[1024,32]{0,1:T(8,128)}, f32[1024,32]{0,1:T(8,128)S(1)}, u32[]{:S(2)}) copy-start(f32[1024,32]{0,1:T(8,128)S(1)} %get-tuple-element.228) | copy-start | bytes 393220
  91.5 14.4 %copy-start.27 = (f32[768]{0:T(1024)}, f32[768]{0:T(1024)S(1)}, u32[]{:S(2)}) copy-start(f32[768]{0:T(1024)S(1)} %get-tuple-element.143) | copy-start | bytes 9220
  91.5 14.4 %copy-start.30 = (f32[768]{0:T(1024)}, f32[768]{0:T(1024)S(1)}, u32[]{:S(2)}) copy-start(f32[768]{0:T(1024)S(1)} %get-tuple-element.142) | copy-start | bytes 9220
  247.4 16.8 %copy-start.1 = (f32[1,1024,768]{2,1,0:T(8,128)S(1)}, f32[1,1024,768]{2,1,0:T(8,128)}, u32[]{:S(2)}) copy-start(f32[1,1024,768]{2,1,0:T(8,128)} %copy-done) | copy-start | bytes 9437188
  247.4 16.8 %copy-start.36 = (bf16[768,3072]{1,0:T(8,128)(2,1)S(1)}, bf16[768,3072]{1,0:T(8,128)(2,1)}, u32[]{:S(2)}) copy-start(bf16[768,3072]{1,0:T(8,128)(2,1)} %all-gather.12.cloned.1.call-done) | copy-start | bytes 14155780
  264.1 5.9 copy-start.7
  264.2 5.9 copy-start.8
  264.2 5.9 copy-start.35
  270.1 10.2 %copy-start.13 = (f32[1024,768]{1,0:T(8,128)}, f32[1024,768]{1,0:T(8,128)S(1)}, u32[]{:S(2)}) copy-start(f32[1024,768]{1,0:T(8,128)S(1)} %get-tuple-element.234) | copy-start | bytes 9437188
  286.6 230.4 %reduce-scatter.6.cloned.1.call-start = ((), (), s32[]{:S(2)}) async-start(), calls=%async_computation.10 | async-start | bytes 2506752 | tf_op jit(solution)/shard_map/reduce_scatter | solution.py:265
  296.0 131.9 %copy-start.16 = (f32[1024,32]{0,1:T(8,128)S(1)}, f32[1024,32]{0,1:T(8,128)}, u32[]{:S(2)}) copy-start(f32[1024,32]{0,1:T(8,128)} %copy-done.15) | copy-start | bytes 393220
  296.0 131.9 %copy-start.18 = (f32[1024,32]{0,1:T(8,128)S(1)}, f32[1024,32]{0,1:T(8,128)}, u32[]{:S(2)}) copy-start(f32[1024,32]{0,1:T(8,128)} %copy-done.17) | copy-start | bytes 393220
  442.8 4.3 copy-start.22
  455.0 155.0 %reduce-scatter.8.cloned.1.call-start = ((), (), s32[]{:S(2)}) async-start(), calls=%async_computation.11 | async-start | bytes 7520256 | tf_op jit(solution)/shard_map/reduce_scatter | solution.py:268
  465.1 259.9 %reduce-scatter.12.cloned.1.call-start = ((), (), s32[]{:S(2)}) async-start(), calls=%async_computation.13 | async-start | bytes 10027008 | tf_op jit(solution)/shard_map/reduce_scatter | solution.py:271
  477.9 361.8 %reduce-scatter.14.cloned.1.call-start = ((), (), s32[]{:S(2)}) async-start(), calls=%async_computation.14 | async-start | bytes 10027008 | tf_op jit(solution)/shard_map/reduce_scatter | solution.py:273
  489.8 423.0 %copy-start.11 = (bf16[128,4608]{1,0:T(8,128)(2,1)S(1)}, bf16[128,4608]{1,0:T(8,128)(2,1)}, u32[]{:S(2)}) copy-start(bf16[128,4608]{1,0:T(8,128)(2,1)} %all-gather.6.cloned.1.call-done) | copy-start | bytes 3538948
  489.8 423.0 %copy-start.33 = (bf16[1,128]{1,0:T(2,128)(2,1)S(1)}, bf16[1,128]{1,0:T(2,128)(2,1)}, u32[]{:S(2)}) copy-start(bf16[1,128]{1,0:T(2,128)(2,1)} %param.21) | copy-start | bytes 772
  489.8 424.5 %all-reduce.18.cloned.1.call-start = ((), (), s32[]{:S(2)}) async-start(), calls=%async_computation.15 | async-start | bytes 1916928 | tf_op jit(solution)/shard_map/psum | solution.py:278
  (16 other events, 47.8 us)
Sparse Core Ops, SparseCore 0:
  10.3 41.2 all-gather.5
  53.8 46.2 all-gather.7
  102.4 36.9 all-gather.9
  141.5 51.9 all-gather.11
  195.7 51.6 all-gather.13
  286.7 61.7 reduce-scatter.9
  455.1 61.8 reduce-scatter.5
  521.0 88.9 reduce-scatter.7
  614.1 110.8 reduce-scatter.11
  728.9 110.7 reduce-scatter.13
  843.5 37.8 all-reduce.17
where the time goes:
time: 941 us; the launch traced here: 929 us
  waiting for transfers between devices  390 us (41%)
  matrix products  278 us (30%)
  blocking collectives  129 us (14%)
  other arithmetic  69.6 us (7%)
  local copies, waits for them, and re-layouts  43 us (5%)
  between operations  18.6 us (2%)
    unnamed x2, blocking collectives  124 us
    reduce_scatter x1, waiting for transfers between devices, shards(): lax.psum_scatter(grad_expander, 'fsdp', scatter_dimension=0, tiled=True)  113 us
    reduce_scatter x1, waiting for transfers between devices, shards(): lax.psum_scatter(grad_contractor, 'fsdp', scatter_dimension=0, tiled=True)  113 us
    reduce_scatter x1, waiting for transfers between devices, shards(): lax.psum_scatter(grad_projector, 'fsdp', scatter_dimension=0, tiled=True)  91.4 us
    dot_general x24, matrix products, head_scores(): jnp.einsum('sqd,skd->sqk', queries, keys, preferred_element_type=jnp.floa...  39.9 us
    all_gather x1, waiting for transfers between devices, shards(): lax.all_gather(contractor, 'fsdp', axis=0, tiled=True)  35.2 us
    dot_general x12, matrix products, attend_head(): jnp.einsum('sqk,skd->sqd', probs, values, preferred_element_type=jnp.floa...  31.3 us
    dot_general x12, matrix products, head_grads(): jnp.einsum('sqk,sqd->skd', probs.astype(jnp.bfloat16), upstream, preferre...  29.7 us
  transfers between devices with their start and end apart: 11, of which 6 were waited for; matrix products, arithmetic and copies ran while one was open for 36% of the time, Pallas kernels for 0%

commit v1 on v0

--- a/solution.py
+++ b/solution.py
@@ -1,3 +1,4 @@
+import functools
 import jax
 import jax.numpy as jnp
 from jax import lax
@@ -6,6 +7,35 @@
 D = 768
 HEADS = 12
 HD = 64
+
+
+def extend_roots(xx, ndim_at):
+    block_now = lax.axis_size("fsdp")
+    carry_out = lax.axis_index("fsdp")
+    n_now, all_rows, step_out = (block_now, carry_out, xx.shape[ndim_at])
+    next_value = map(lambda src_i: (src_i, (src_i + 1) % n_now), range(n_now))
+    sides = list(next_value)
+    after = range(n_now)
+    base_arr = map(lambda src_i: (src_i, (src_i - 1) % n_now), after)
+    runs = list(base_arr)
+    z_new = jnp.zeros((*xx.shape[:ndim_at], n_now * step_out, *xx.shape[ndim_at + 1 :]), xx.dtype)
+    z_new = lax.dynamic_update_slice_in_dim(z_new, xx, all_rows * step_out, axis=ndim_at)
+    low = parts_out = xx
+    t_next = n_now // 2
+    for dev in range(1, t_next + 1):
+        low = lax.ppermute(low, "fsdp", sides)
+        z_new = lax.dynamic_update_slice_in_dim(
+            z_new, low, (all_rows - dev) % n_now * step_out, axis=ndim_at
+        )
+        if dev < n_now - t_next:
+            parts_out = lax.ppermute(parts_out, "fsdp", runs)
+            z_new = lax.dynamic_update_slice_in_dim(
+                z_new, parts_out, (all_rows + dev) % n_now * step_out, axis=ndim_at
+            )
+    return z_new
+
+
+_prepare_digits = functools.partial(extend_roots, ndim_at=0)
 
 
 def norm_shift(values, gain, shift, scale):
@@ -97,7 +127,7 @@
         lax.all_gather(midscale, "fsdp", axis=0, tiled=True),
         lax.all_gather(expander, "fsdp", axis=0, tiled=True),
         lax.all_gather(thresholds, "fsdp", axis=0, tiled=True),
-        lax.all_gather(contractor, "fsdp", axis=0, tiled=True),
+        _prepare_digits(contractor),
         lax.all_gather(baseline, "fsdp", axis=0, tiled=True),
         lax.all_gather(absorber, "fsdp", axis=0, tiled=True),
     )

time: 941 us -> 961 us (1.021)
  starting transfers between devices: 0.61 us -> 33.9 us
  waiting for transfers between devices: 390 us -> 365 us
  local copies, waits for them, and re-layouts: 43 us -> 55.2 us
    all_gather x1, waiting for transfers between devices: 35.2 us -> 0.01 us  [shards(): lax.all_gather(contractor, 'fsdp', axis=0, tiled=True)]
    ppermute x0 -> x15, starting transfers between devices: none -> 33.2 us  [the longest x7 32.6 us: extend_roots(): parts_out = lax.ppermute(parts_out, 'fsdp', runs)]
    ppermute x0 -> x15, waiting for transfers between devices: none -> 20.5 us  [the longest x7 13.3 us: extend_roots(): parts_out = lax.ppermute(parts_out, 'fsdp', runs)]
    dynamic_update_slice x0 -> x16, local copies, waits for them, and re-layouts: none -> 11.7 us  [the longest x8 5.86 us: extend_roots(): lax.dynamic_update_slice_in_dim(z_new, low, (all_rows - dev) % n_now * st...]
  transfers between devices with their start and end apart: 11 -> 26, of which waited for: 6 -> 15; matrix products, arithmetic and copies ran while one was open for 36% -> 37% of each run, Pallas kernels for 0% -> 0%
where the time goes in v1:
time: 961 us; the launch traced here: 952 us
  waiting for transfers between devices  365 us (38%)
  matrix products  280 us (29%)
  blocking collectives  124 us (13%)
  other arithmetic  74.1 us (8%)
  local copies, waits for them, and re-layouts  55.2 us (6%)
  starting transfers between devices  33.9 us (4%)
  between operations  19 us (2%)
    unnamed x2, blocking collectives  119 us
    reduce_scatter x1, waiting for transfers between devices, shards(): lax.psum_scatter(grad_expander, 'fsdp', scatter_dimension=0, tiled=True)  113 us
    reduce_scatter x1, waiting for transfers between devices, shards(): lax.psum_scatter(grad_contractor, 'fsdp', scatter_dimension=0, tiled=True)  113 us
    reduce_scatter x1, waiting for transfers between devices, shards(): lax.psum_scatter(grad_projector, 'fsdp', scatter_dimension=0, tiled=True)  91.3 us
    dot_general x24, matrix products, head_scores(): jnp.einsum('sqd,skd->sqk', queries, keys, preferred_element_type=jnp.floa...  40 us
    ppermute x7, starting transfers between devices, extend_roots(): parts_out = lax.ppermute(parts_out, 'fsdp', runs)  32.6 us
    dot_general x12, matrix products, attend_head(): jnp.einsum('sqk,skd->sqd', probs, values, preferred_element_type=jnp.floa...  31.2 us
    dot_general x12, matrix products, head_grads(): jnp.einsum('sqk,sqd->skd', probs.astype(jnp.bfloat16), upstream, preferre...  29.7 us
  transfers between devices with their start and end apart: 26, of which 15 were waited for; matrix products, arithmetic and copies ran while one was open for 37% of the time, Pallas kernels for 0%

profile of v1, /device:TPU:0, one launch (start us, length us, event | category | flops | bytes accessed | tf_op | source)
XLA Modules:
  0.0 951.9 jit_solution(9550767468117868754)
XLA Ops:
  10.6 5.0 collective-permute-start.1
  24.1 58.8 %all-reduce.13 = (bf16[4608]{0:T(1024)(128)(2,1)S(1)}, bf16[768]{0:T(1024)(128)(2,1)S(1)}, bf16[768]{0:T(1024)(128)(2,1)S(1)}, bf16[768]{0:T(1024)(128)(2,1)S(1)...) all-reduce(bf16[4608]{0:T(1024)(128)(2,1)S(1)} %dynamic-update-slic, ...), channel_id=1, replica_groups=mesh['dp'=2,'fsdp'=16] {'fsdp'}, use_global_device_ids=true, to_apply=%add.1 | all-reduce | flops 10752 | bytes 43008
  91.3 4.5 collective-permute-start.3
  101.0 4.7 collective-permute-start.5
  109.9 4.6 collective-permute-start.7
  119.5 4.6 collective-permute-start.9
  129.0 4.6 collective-permute-start.11
  139.5 4.6 collective-permute-start.13
  155.8 5.9 copy.43
  161.8 6.4 fusion.74
  176.7 4.1 copy.46
  180.8 4.3 copy.47
  185.0 60.4 %while.28 = (s32[]{:T(128)}, bf16[12,1,1024,64]{2,3,1,0:T(8,128)(2,1)}, f32[12,1,1024]{2,1,0:T(1,128)S(1)}, bf16[12,1,1024,64]{3,2,1,0:T(8,128)(2,1)S(1)}, bf16[...) while((s32[]{:T(128)}, bf16[12,1,1024,64]{2,3,1,0:T(8,128)(2,1)}, ...), condition=%wide.region_5.6_spmd.clone, body=%wide.region_2.5_spmd.sunk.clone | while | flops 277871616 | bytes 13674569 | solution.py:176
  245.5 5.6 fusion.102
  253.3 15.2 %multiply_convert_fusion.1 = (bf16[1024,3072]{1,0:T(8,128)(2,1)}, f32[1024,3072]{1,0:T(8,128)}) fusion(f32[3072]{0:T(1024)S(1)} %convert_element_type.211, bf16[768,3072]{1,0:T(8,128)(2,1)} %all-gather.12.cloned.1.call-done, f32[1,1024,768]{2,1,0:T(8,128)} %copy-done, f32[768]{0:T(1024)S(1)} %get-tuple-element.140, f32[768]{0:T(1024)S(1)} %get-tuple-element.141, ...), kind=kOutput, calls=%fused_computation.65 | convolution fusion | flops 4868014080 | bytes 26768384 | tf_op jit(solution)/shard_map/dot_general | solution.py:186
  268.5 16.7 %convert_reduce_fusion = (f32[3072]{0:T(1024)S(1)}, bf16[1024,3072]{1,0:T(8,128)(2,1)S(1)}) fusion(f32[1024,3072]{1,0:T(8,128)} %get-tuple-element.233, f32[3072]{0:T(1024)S(1)} %convert_element_type.211, bf16[3072,768]{1,0:T(8,128)(2,1)} %all-gather.14.cloned.1.call-done, bf16[1,1024,768]{2,1,0:T(8,128)(2,1)} %param.35, f32[768]{0:T(1024)S(1)} %get-tuple-element.139), kind=kOutput, calls=%fused_computation.64 | convolution fusion | flops 4906546176 | bytes 25193472 | tf_op jit(solution)/shard_map/td,fd->tf/dot_general | solution.py:226
  285.3 5.9 fusion.58
  291.2 10.7 %fusion.57 = (f32[768]{0:T(1024)S(1)}, bf16[1,1024,768]{2,1,0:T(8,128)(2,1)}, f32[1024]{0:T(1024)S(1)}, f32[1,1024,768]{2,1,0:T(8,128)S(1)}) fusion(bf16[1,1024,768]{2,1,0:T(8,128)(2,1)S(1)} %copy-done.6, f32[768]{0:T(1024)S(1)} %convert_element_type.213, f32[1,1024,768]{2,1,0:T(8,128)S(1)} %copy-done.1, f32[768]{0:T(1024)S(1)} %get-tuple-element.139, ...), kind=kOutput, calls=%fused_computation.73 | convolution fusion | flops 4843632640 | bytes 23624704 | tf_op jit(solution)/shard_map/dot_general | solution.py:190
  303.9 5.1 fusion.81
  309.2 4.8 convolution_convert_fusion
  313.9 4.4 copy.48
  318.3 131.9 %while.29 = (s32[]{:T(128)}, f32[12,1,1024,64]{2,3,1,0:T(8,128)}, f32[12,1,1024,64]{2,3,1,0:T(8,128)}, bf16[12,1,1024,64]{2,3,1,0:T(8,128)(2,1)}, bf16[12,1,1024...) while((s32[]{:T(128)}, f32[12,1,1024,64]{2,3,1,0:T(8,128)}, ...), condition=%wide.region_12.13_spmd.clone, body=%wide.region_10.12_spmd.sunk.clone | while | flops 683801600 | bytes 34112608 | solution.py:250
  458.5 6.7 fusion.59
  478.6 9.8 %fusion.76 = f32[768,2304]{1,0:T(8,128)} fusion(bf16[1024,2304]{0,1:T(8,128)(2,1)} %bitcast.248, bf16[1,1024,768]{2,1,0:T(8,128)(2,1)S(1)} %copy-done.4, f32[768]{0:T(1024)S(1)} %copy-done.30, f32[768]{0:T(1024)S(1)} %copy-done.27, f32[768]{0:T(1024)S(1)} %copy-done.23, f32[1024]{0:T(1024)S(1)} %copy-done.25, f32[1024]{0:T(1024)S(1)} %copy-done.19, ...), kind=kOutput, calls=%fused_computation.118 | convolution fusion | flops 3630170112 | bytes 13390848 | tf_op jit(solution)/shard_map/td,te->de/dot_general | solution.py:261
  490.4 10.9 %fusion.96 = f32[768,3072]{1,0:T(8,128)} fusion(bf16[1024,3072]{1,0:T(8,128)(2,1)} %copy-done.5, f32[1,1024,768]{2,1,0:T(8,128)S(1)} %copy-done.2, f32[768]{0:T(1024)S(1)} %get-tuple-element.140, f32[768]{0:T(1024)S(1)} %get-tuple-element.141, f32[768]{0:T(1024)S(1)} %convert_element_type.209, f32[1024]{0:T(1024)S(1)} %fusion.87, ...), kind=kOutput, calls=%fused_computation.194 | convolution fusion | flops 4836556800 | bytes 18891776 | tf_op jit(solution)/shard_map/td,tf->df/dot_general | solution.py:232
  502.7 10.5 %fusion.78 = f32[3072,768]{1,0:T(8,128)} fusion(bf16[1024,3072]{1,0:T(8,128)(2,1)} %get-tuple-element.232, bf16[1,1024,768]{2,1,0:T(8,128)(2,1)S(1)} %copy-done.7, f32[768]{0:T(1024)S(1)} %get-tuple-element.139), kind=kOutput, calls=%fused_computation.129 | convolution fusion | flops 4834197504 | bytes 17304576 | tf_op jit(solution)/shard_map/tf,td->fd/dot_general | solution.py:223
  515.0 24.2 %reduce-scatter.6.cloned.1.call-done = f32[8,4608]{1,0:T(8,128)} async-done(((f32[128,4608]{1,0:T(8,128)}), f32[8,4608]{1,0:T(8,128)}) %reduce-scatter.6.cloned.1.call-update) | async-done | bytes 147472 | tf_op jit(solution)/shard_map/reduce_scatter | solution.py:295
  540.7 91.3 %reduce-scatter.8.cloned.1.call-done = f32[48,2304]{1,0:T(8,128)} async-done(((f32[768,2304]{1,0:T(8,128)}), f32[48,2304]{1,0:T(8,128)}) %reduce-scatter.8.cloned.1.call-update) | async-done | bytes 442384 | tf_op jit(solution)/shard_map/reduce_scatter | solution.py:298
  633.8 113.3 %reduce-scatter.12.cloned.1.call-done = f32[48,3072]{1,0:T(8,128)} async-done(((f32[768,3072]{1,0:T(8,128)}), f32[48,3072]{1,0:T(8,128)}) %reduce-scatter.12.cloned.1.call-update) | async-done | bytes 589840 | tf_op jit(solution)/shard_map/reduce_scatter | solution.py:301
  748.9 113.0 %reduce-scatter.14.cloned.1.call-done = f32[192,768]{1,0:T(8,128)} async-done(((f32[3072,768]{1,0:T(8,128)}), f32[192,768]{1,0:T(8,128)}) %reduce-scatter.14.cloned.1.call-update) | async-done | bytes 589840 | tf_op jit(solution)/shard_map/reduce_scatter | solution.py:303
  866.1 60.3 %all-reduce.12 = (bf16[4608]{0:T(1024)(128)(2,1)S(1)}, bf16[768]{0:T(1024)(128)(2,1)S(1)}, bf16[768]{0:T(1024)(128)(2,1)S(1)}, bf16[3072]{0:T(1024)(128)(2,1)S(1...) all-reduce(f32[4608]{0:T(1024)S(1)} %reduce.32, ...), channel_id=3, replica_groups=mesh['dp'=2,'fsdp'=16] {'fsdp'}, use_global_device_ids=true, to_apply=%region_23.24.clone | all-reduce | flops 10752 | bytes 64512
  926.8 4.9 all-reduce.14
  (375 shorter events, 307.0 us)
Async XLA Ops:
  7.2 142.4 %all-gather.6.cloned.1.call-start = ((), (), s32[]{:S(2)}) async-start(), calls=%async_computation.5 | async-start | bytes 1253376 | tf_op jit(solution)/shard_map/all_gather | solution.py:122
  7.9 147.9 %all-gather.8.cloned.1.call-start = ((), (), s32[]{:S(2)}) async-start(), calls=%async_computation.6 | async-start | bytes 3760128 | tf_op jit(solution)/shard_map/all_gather | solution.py:125
  8.7 236.8 %all-gather.10.cloned.1.call-start = ((), (), s32[]{:S(2)}) async-start(), calls=%async_computation.7 | async-start | bytes 1253376 | tf_op jit(solution)/shard_map/all_gather | solution.py:126
  9.4 243.9 %all-gather.12.cloned.1.call-start = ((), (), s32[]{:S(2)}) async-start(), calls=%async_computation.8 | async-start | bytes 5013504 | tf_op jit(solution)/shard_map/all_gather | solution.py:128
  10.0 258.5 %all-gather.14.cloned.1.call-start = ((), (), s32[]{:S(2)}) async-start(), calls=%async_computation.9 | async-start | bytes 5013504 | tf_op jit(solution)/shard_map/all_gather | solution.py:202
  10.0 77.0 %collective-permute-start = (bf16[192,768]{1,0:T(8,128)(2,1)}, bf16[192,768]{1,0:T(8,128)(2,1)S(1)}, u32[]{:S(2)}, u32[]{:S(2)}) collective-permute-start(bf16[192,768]{1,0:T(8,128)(2,1)} %param.32), channel_id=1, source_target_pairs={{0,1},{1,2},{2,3},{3,4},{4,5},{5,6},{6,7},{7,8},{8,9},{9,10},{10,1... | collective-permute-start | bytes 884744 | tf_op jit(solution)/shard_map/ppermute | solution.py:26
  10.6 80.7 %collective-permute-start.1 = (bf16[192,768]{1,0:T(8,128)(2,1)}, bf16[192,768]{1,0:T(8,128)(2,1)S(1)}, u32[]{:S(2)}, u32[]{:S(2)}) collective-permute-start(bf16[192,768]{1,0:T(8,128)(2,1)} %param.32), channel_id=1, source_target_pairs={{0,15},{1,0},{2,1},{3,2},{4,3},{5,4},{6,5},{7,6},{8,7},{9,8},{10,9... | collective-permute-start | bytes 884744 | tf_op jit(solution)/shard_map/ppermute | solution.py:31
  15.7 497.7 %reduce-scatter.10.cloned.1.call-start = ((), (), s32[]{:S(2)}) async-start(), calls=%async_computation.12 | async-start | bytes 2506752 | tf_op jit(solution)/shard_map/reduce_scatter | solution.py:299
  87.0 83.5 %copy-start.13 = (f32[1024,32]{0,1:T(8,128)}, f32[1024,32]{0,1:T(8,128)S(1)}, u32[]{:S(2)}) copy-start(f32[1024,32]{0,1:T(8,128)S(1)} %get-tuple-element.227) | copy-start | bytes 393220
  87.0 83.5 %copy-start.15 = (f32[1024,32]{0,1:T(8,128)}, f32[1024,32]{0,1:T(8,128)S(1)}, u32[]{:S(2)}) copy-start(f32[1024,32]{0,1:T(8,128)S(1)} %get-tuple-element.228) | copy-start | bytes 393220
  87.0 10.6 %collective-permute-start.2 = (bf16[192,768]{1,0:T(8,128)(2,1)S(1)}, bf16[192,768]{1,0:T(8,128)(2,1)S(1)}, u32[]{:S(2)}, u32[]{:S(2)}) collective-permute-start(bf16[192,768]{1,0:T(8,128)(2,1)S(1)} %collective-permute-done), channel_id=1, source_target_pairs={{0,1},{1,2},{2,3},{3,4},{4,5},{5,6},{6,7},{7,8},{8,9},{9,10},{10,1... | collective-permute-start | bytes 884744 | tf_op jit(solution)/shard_map/ppermute | solution.py:26
  91.3 9.7 %collective-permute-start.3 = (bf16[192,768]{1,0:T(8,128)(2,1)S(1)}, bf16[192,768]{1,0:T(8,128)(2,1)S(1)}, u32[]{:S(2)}, u32[]{:S(2)}) collective-permute-start(bf16[192,768]{1,0:T(8,128)(2,1)S(1)} %collective-permute-done.1), channel_id=1, source_target_pairs={{0,15},{1,0},{2,1},{3,2},{4,3},{5,4},{6,5},{7,6},{8,7},{9,8},{10,9... | collective-permute-start | bytes 884744 | tf_op jit(solution)/shard_map/ppermute | solution.py:31
  97.6 9.1 collective-permute-start.4
  101.0 8.9 collective-permute-start.5
  106.8 9.2 collective-permute-start.6
  109.9 9.6 %collective-permute-start.7 = (bf16[192,768]{1,0:T(8,128)(2,1)S(1)}, bf16[192,768]{1,0:T(8,128)(2,1)S(1)}, u32[]{:S(2)}, u32[]{:S(2)}) collective-permute-start(bf16[192,768]{1,0:T(8,128)(2,1)S(1)} %collective-permute-done.5), channel_id=1, source_target_pairs={{0,15},{1,0},{2,1},{3,2},{4,3},{5,4},{6,5},{7,6},{8,7},{9,8},{10,9... | collective-permute-start | bytes 884744 | tf_op jit(solution)/shard_map/ppermute | solution.py:31
  116.0 9.7 %collective-permute-start.8 = (bf16[192,768]{1,0:T(8,128)(2,1)S(1)}, bf16[192,768]{1,0:T(8,128)(2,1)S(1)}, u32[]{:S(2)}, u32[]{:S(2)}) collective-permute-start(bf16[192,768]{1,0:T(8,128)(2,1)S(1)} %collective-permute-done.6), channel_id=1, source_target_pairs={{0,1},{1,2},{2,3},{3,4},{4,5},{5,6},{6,7},{7,8},{8,9},{9,10},{10,1... | collective-permute-start | bytes 884744 | tf_op jit(solution)/shard_map/ppermute | solution.py:26
  119.5 9.5 collective-permute-start.9
  125.7 9.3 collective-permute-start.10
  129.0 10.5 %collective-permute-start.11 = (bf16[192,768]{1,0:T(8,128)(2,1)S(1)}, bf16[192,768]{1,0:T(8,128)(2,1)S(1)}, u32[]{:S(2)}, u32[]{:S(2)}) collective-permute-start(bf16[192,768]{1,0:T(8,128)(2,1)S(1)} %collective-permute-done.9), channel_id=1, source_target_pairs={{0,15},{1,0},{2,1},{3,2},{4,3},{5,4},{6,5},{7,6},{8,7},{9,8},{10,9... | collective-permute-start | bytes 884744 | tf_op jit(solution)/shard_map/ppermute | solution.py:31
  135.0 11.2 %collective-permute-start.12 = (bf16[192,768]{1,0:T(8,128)(2,1)S(1)}, bf16[192,768]{1,0:T(8,128)(2,1)S(1)}, u32[]{:S(2)}, u32[]{:S(2)}) collective-permute-start(bf16[192,768]{1,0:T(8,128)(2,1)S(1)} %collective-permute-done.10), channel_id=1, source_target_pairs={{0,1},{1,2},{2,3},{3,4},{4,5},{5,6},{6,7},{7,8},{8,9},{9,10},{10,1... | collective-permute-start | bytes 884744 | tf_op jit(solution)/shard_map/ppermute | solution.py:26
  139.5 9.3 collective-permute-start.13
  146.3 8.8 collective-permute-start.14
  309.1 230.1 %reduce-scatter.6.cloned.1.call-start = ((), (), s32[]{:S(2)}) async-start(), calls=%async_computation.10 | async-start | bytes 2506752 | tf_op jit(solution)/shard_map/reduce_scatter | solution.py:295
  318.3 131.9 %copy-start.14 = (f32[1024,32]{0,1:T(8,128)S(1)}, f32[1024,32]{0,1:T(8,128)}, u32[]{:S(2)}) copy-start(f32[1024,32]{0,1:T(8,128)} %copy-done.13) | copy-start | bytes 393220
  318.3 131.9 %copy-start.16 = (f32[1024,32]{0,1:T(8,128)S(1)}, f32[1024,32]{0,1:T(8,128)}, u32[]{:S(2)}) copy-start(f32[1024,32]{0,1:T(8,128)} %copy-done.15) | copy-start | bytes 393220
  478.3 153.8 %reduce-scatter.8.cloned.1.call-start = ((), (), s32[]{:S(2)}) async-start(), calls=%async_computation.11 | async-start | bytes 7520256 | tf_op jit(solution)/shard_map/reduce_scatter | solution.py:298
  488.5 258.6 %reduce-scatter.12.cloned.1.call-start = ((), (), s32[]{:S(2)}) async-start(), calls=%async_computation.13 | async-start | bytes 10027008 | tf_op jit(solution)/shard_map/reduce_scatter | solution.py:301
  501.3 360.6 %reduce-scatter.14.cloned.1.call-start = ((), (), s32[]{:S(2)}) async-start(), calls=%async_computation.14 | async-start | bytes 10027008 | tf_op jit(solution)/shard_map/reduce_scatter | solution.py:303
  513.3 421.7 %copy-start.9 = (bf16[128,4608]{1,0:T(8,128)(2,1)S(1)}, bf16[128,4608]{1,0:T(8,128)(2,1)}, u32[]{:S(2)}) copy-start(bf16[128,4608]{1,0:T(8,128)(2,1)} %all-gather.6.cloned.1.call-done) | copy-start | bytes 3538948
  513.3 421.7 %copy-start.32 = (bf16[1,128]{1,0:T(2,128)(2,1)S(1)}, bf16[1,128]{1,0:T(2,128)(2,1)}, u32[]{:S(2)}) copy-start(bf16[1,128]{1,0:T(2,128)(2,1)} %param.21) | copy-start | bytes 772
  513.3 423.2 %all-reduce.18.cloned.1.call-start = ((), (), s32[]{:S(2)}) async-start(), calls=%async_computation.15 | async-start | bytes 1916928 | tf_op jit(solution)/shard_map/psum | solution.py:308
  (30 other events, 538.0 us)
Sparse Core Ops, SparseCore 0:
  10.3 41.1 all-gather.5
  53.8 55.2 all-gather.7
  111.3 41.8 all-gather.9
  155.4 51.8 all-gather.11
  209.5 51.6 all-gather.13
  309.2 60.8 reduce-scatter.9
  478.4 60.7 reduce-scatter.5
  543.2 88.8 reduce-scatter.7
  636.2 110.8 reduce-scatter.11
  751.1 110.8 reduce-scatter.13
  865.7 37.8 all-reduce.17
